TPU v7x, 256 devices: a whole 4x4x8 slice. The times are simulated.
256 devices in a mesh: dp: 8 (over z), vocab: 32 (over x, y, core).
Axes of the slice: x: 4, y: 4, z: 8, core: 2. Of those that a mesh axis runs over, the one named last changes fastest.
Arguments:
- hidden: bfloat16 [8, 2, 64, 4608], P('dp'), may hold values from -6 to 6
- table: bfloat16 [73728, 4608], P('vocab', 'dp'), may hold values from -0.25 to 0.25
- new_mask: int32 [73728], P('vocab'), may hold values from 0 to 1, as said below
- labels: int32 [8, 2, 64], P('dp'), may hold values from 0 to 73727
- in_grad: bfloat16 [8, 2, 768, 4608], P('dp', None, 'vocab'), may hold values from -0.75 to 0.75
- item_owner: int32 [8, 2, 768, 1], P('dp', None, 'vocab'), may hold values from 0 to 31; in each aligned block of 24 rows (0 to 23, 24 to 47, ..., all dimensions but the last counted through in order) at most 2 rows name the same one
- item_slot: int32 [8, 2, 768], P('dp', None, 'vocab'), may hold values from 0 to 255
- first_moment: float32 [8192, 4608], P('vocab', 'dp'), may hold values from -0.75 to 0.75
- second_moment: float32 [8192, 4608], P('vocab', 'dp'), may hold values from 0.0001 to 0.01
Outputs:
- token_loss: float32 [8, 2, 64], P('dp')
- d_hidden: bfloat16 [8, 2, 64, 4608], P('dp', None, None, 'vocab')
- update: float32 [8192, 4608], P('vocab', 'dp')
- first_out: float32 [8192, 4608], P('vocab', 'dp')
- second_out: float32 [8192, 4608], P('vocab', 'dp')
Inputs may be any that keep to these rules, and one draw needn't show every extreme that they name: `new_mask`: each aligned block of 2304 entries holds exactly 256 ones. `item_owner`: within the 24 rows of one device in one block, no shard is named more than 2 times, a bound that some block reaches.
All inputs are finite; a program needn't handle non-finite values.
Results may differ from a plain program's by a relative error of at most 0.006.
Values may be sent and summed in bfloat16 or wider, within the bound.
No kernel may reach another device: no remote copies, remote signals or barrier semaphores. Data moves between devices by JAX's collectives and lax.ppermute only.
A program may use at most 128 MiB of HBM per device.

v0:
```python
import jax
import jax.numpy as jnp
from jax import lax
from jax.experimental import pallas as pl
from jax.experimental.pallas import tpu as pltpu
from jax.sharding import PartitionSpec as P


cap_value = 30.0
beta_one = 0.9
beta_two = 0.95
step_count = 10
epsilon = 1e-08
decay_rate = 0.1


def sent_to_all(array, axis):
    peers = lax.axis_size(axis)
    return lax.all_to_all(
        jnp.broadcast_to(array[None], (peers, *array.shape)), axis, 0, 0, tiled=True
    )


def exchanged(parts, axis):
    return lax.all_to_all(parts, axis, split_axis=0, concat_axis=0, tiled=True)


def as_digits(numbers):
    return jnp.stack([numbers & 255, (numbers >> 8) & 255, numbers >> 16]).astype(jnp.bfloat16)


def from_digits(digits):
    low, middle, high = (digits[k].astype(jnp.int32) for k in range(3))
    return low + (middle << 8) + (high << 16)


def forward_kernel(first_row_ref, part_ref, states_ref, label_ref, weight_ref, sums_ref, raw_ref):
    step = pl.program_id(0)
    product = jnp.dot(part_ref[0], states_ref[...], preferred_element_type=jnp.float32)

    @pl.when(step == 0)
    def _():
        raw_ref[...] = product

    @pl.when(step > 0)
    def _():
        raw_ref[...] += product

    @pl.when(step == pl.num_programs(0) - 1)
    def _():
        rows, tokens = raw_ref.shape
        strip = 16
        labels = label_ref[...]

        def one_strip(k, carry):
            total, pick = carry
            at = pl.ds(pl.multiple_of(k * strip, strip), strip)
            squashed = jnp.tanh(raw_ref[at, :] * (1.0 / cap_value))
            capped = cap_value * squashed
            expd = jnp.exp(capped)
            ids = (
                lax.broadcasted_iota(jnp.int32, (strip, tokens), 0) + first_row_ref[0] + k * strip
            )
            weight_ref[at, :] = (expd * (1.0 - squashed * squashed)).astype(weight_ref.dtype)
            picked = jnp.where(ids == labels, capped, 0.0)
            for half in range(0, strip, 8):
                total = total + expd[half : half + 8]
                pick = pick + picked[half : half + 8]
            return total, pick

        zero = jnp.zeros((8, tokens), jnp.float32)
        total, pick = lax.fori_loop(0, rows // strip, one_strip, (zero, zero))
        sums_ref[0:1, :] = jnp.sum(total, axis=0, keepdims=True)
        sums_ref[1:2, :] = jnp.sum(pick, axis=0, keepdims=True)


def forward_block(whole, states, label_row, first_row):
    parts, rows, columns = whole.shape
    tokens = states.shape[1]
    return pl.pallas_call(
        forward_kernel,
        grid=(parts,),
        in_specs=[
            pl.BlockSpec(memory_space=pltpu.SMEM),
            pl.BlockSpec((1, rows, columns), lambda k: (k, 0, 0)),
            pl.BlockSpec((columns, tokens), lambda k: (k, 0)),
            pl.BlockSpec((1, tokens), lambda k: (0, 0)),
        ],
        out_specs=[
            pl.BlockSpec((rows, tokens), lambda k: (0, 0)),
            pl.BlockSpec((2, tokens), lambda k: (0, 0)),
        ],
        out_shape=[
            jax.ShapeDtypeStruct((rows, tokens), jnp.bfloat16),
            jax.ShapeDtypeStruct((2, tokens), jnp.float32),
        ],
        scratch_shapes=[pltpu.VMEM((rows, tokens), jnp.float32)],
        compiler_params=pltpu.CompilerParams(dimension_semantics=("arbitrary",)),
        cost_estimate=pl.CostEstimate(
            flops=2 * parts * rows * columns * tokens,
            bytes_accessed=2 * parts * columns * (rows + tokens),
            transcendentals=2 * rows * tokens,
        ),
        name="forward_block",
    )(first_row.reshape(1), whole, states, label_row.reshape(1, tokens))


def select_rows(new_mask, new_count):
    ranked = jnp.cumsum(new_mask) - 1
    wanted = (ranked[None, :] == jnp.arange(new_count, dtype=jnp.int32)[:, None]) & (
        new_mask[None, :] == 1
    )
    return wanted.astype(jnp.bfloat16)


def pack_items(arrived, columns, sets, shards, capacity):
    rows = arrived.reshape(-1, arrived.shape[2])
    owner = rows[:, columns].astype(jnp.int32).reshape(sets, -1)
    earlier = jnp.tril(jnp.ones((owner.shape[1], owner.shape[1]), jnp.bool_), -1)
    ranked = jnp.sum(
        ((owner[:, :, None] == owner[:, None, :]) & earlier[None]).astype(jnp.int32), axis=2
    )
    place = (owner * sets + jnp.arange(sets, dtype=jnp.int32)[:, None]) * capacity + ranked
    held = shards * sets * capacity
    placing = jnp.arange(held, dtype=jnp.int32)[:, None] == place.reshape(1, -1)
    sent = jnp.dot(placing.astype(jnp.bfloat16), rows, preferred_element_type=jnp.float32)
    return sent.astype(jnp.bfloat16).reshape(shards, sets * capacity, -1)


def body(
    hidden, table, new_mask, labels, in_grad, item_owner, item_slot, first_moment, second_moment
):
    blocks, span, width = hidden.shape[1:]
    tokens = blocks * span
    new_count = first_moment.shape[0]
    rows, columns = table.shape
    groups = lax.axis_size("dp")
    shards = lax.axis_size("vocab")
    group = lax.axis_index("dp")
    shard = lax.axis_index("vocab")
    piece = width // shards
    total_tokens = groups * tokens
    row_part = rows // groups
    items_here = in_grad.shape[2]
    capacity = max(2, (2 * items_here + shards - 1) // shards)

    own = lax.dynamic_slice(
        hidden[0].reshape(tokens, width), (0, shard * piece), (tokens, piece)
    ).T
    digits = jnp.pad(as_digits(labels[0].reshape(tokens)), ((0, 13), (0, 0)))
    arrived = sent_to_all(jnp.concatenate([own, digits], axis=0), "dp")
    slices = arrived[:, :piece].transpose(1, 0, 2).reshape(piece, total_tokens)
    states = lax.all_gather(slices, "vocab", axis=0, tiled=True)
    label_row = from_digits(arrived[:, piece : piece + 3].transpose(1, 0, 2)).reshape(total_tokens)

    whole = exchanged(table.reshape(groups, row_part, columns), "dp")

    items = blocks * items_here
    item_columns = in_grad[0].reshape(items, groups, columns).transpose(1, 0, 2)
    lane = jnp.arange(64, dtype=jnp.int32)[None, :]
    marks = jnp.where(
        lane == 0,
        item_owner[0].reshape(items, 1),
        jnp.where(lane == 1, item_slot[0].reshape(items, 1) + 1, 0),
    ).astype(jnp.bfloat16)
    item_columns = jnp.concatenate(
        [item_columns, jnp.broadcast_to(marks[None], (groups, items, 64))], axis=2
    )
    whole, item_columns = lax.optimization_barrier((whole, item_columns))

    weights, local_sums = forward_block(
        whole, states, label_row, shard * rows + group * row_part
    )
    all_weights = lax.all_gather(weights, "dp", axis=0, tiled=True)

    sums = local_sums.reshape(-1, tokens)
    sums = sent_to_all(sums, "vocab").sum(axis=0)
    sums = sent_to_all(sums, "dp").sum(axis=0).reshape(2, total_tokens)
    total, picked = sums[0], sums[1]
    loss = lax.dynamic_slice(
        (jnp.log(total) - picked).reshape(groups, tokens), (group, 0), (1, tokens)
    )
    item_columns = exchanged(item_columns, "dp")
    sent_rows = pack_items(item_columns, columns, groups * blocks, shards, capacity)
    got_rows = exchanged(sent_rows, "vocab").reshape(-1, columns + 64)
    targets = got_rows[:, columns + 1].astype(jnp.int32) - 1

    inverse = 1.0 / total
    label_weight = (
        (jnp.exp(picked) - total) * (1.0 - (picked / cap_value) ** 2)
    ).astype(jnp.bfloat16)
    shard_rows = shard * rows + jnp.arange(rows, dtype=jnp.int32)
    error = jnp.where(
        shard_rows[:, None] == label_row[None, :], label_weight[None, :], all_weights
    )

    partial_states = (
        lax.dot_general(
            table, error, (((0,), (0,)), ((), ())), preferred_element_type=jnp.float32
        )
        * inverse[None, :]
    ).astype(jnp.bfloat16)
    split = shards // groups
    parts = (
        partial_states.reshape(split, columns // split, groups, tokens)
        .transpose(2, 0, 1, 3)
        .reshape(shards, columns // split, tokens)
    )
    d_states = exchanged(parts, "vocab").astype(jnp.float32).sum(axis=0).astype(jnp.bfloat16)
    d_states = lax.ppermute(
        d_states,
        ("dp", "vocab"),
        [
            (z * shards + g * split + s, g * shards + z * split + s)
            for z in range(groups)
            for g in range(groups)
            for s in range(split)
        ],
    )
    d_hidden = d_states.T.reshape(1, blocks, span, columns // split)

    select = select_rows(new_mask, new_count)
    params = jnp.dot(select, table, preferred_element_type=jnp.float32)
    chosen = (
        jnp.dot(select, error, preferred_element_type=jnp.float32) * inverse[None, :]
    ).astype(jnp.bfloat16)
    own_states = lax.dynamic_slice(states, (group * columns, 0), (columns, total_tokens))
    grads = lax.dot_general(
        chosen, own_states, (((1,), (1,)), ((), ())), preferred_element_type=jnp.float32
    )
    picking = (jnp.arange(new_count, dtype=jnp.int32)[:, None] == targets[None, :]).astype(
        jnp.bfloat16
    )
    grads = grads + jnp.dot(
        picking, got_rows[:, :columns], preferred_element_type=jnp.float32
    )
    first_out = beta_one * first_moment + (1.0 - beta_one) * grads
    second_out = beta_two * second_moment + (1.0 - beta_two) * grads * grads
    update = (
        first_out
        / (1.0 - beta_one**step_count)
        / (jnp.sqrt(second_out / (1.0 - beta_two**step_count)) + epsilon)
        + decay_rate * params
    )
    return (loss.reshape(1, blocks, span), d_hidden, update, first_out, second_out)


def solution(mesh):
    return jax.shard_map(
        body,
        mesh=mesh,
        in_specs=(
            P("dp", None, None, None),
            P("vocab", "dp"),
            P("vocab"),
            P("dp", None, None),
            P("dp", None, "vocab", None),
            P("dp", None, "vocab", None),
            P("dp", None, "vocab"),
            P("vocab", "dp"),
            P("vocab", "dp"),
        ),
        out_specs=(
            P("dp", None, None),
            P("dp", None, None, "vocab"),
            P("vocab", "dp"),
            P("vocab", "dp"),
            P("vocab", "dp"),
        ),
        check_vma=False,
    )
```

profile of v0, /device:TPU:38, one launch (start us, length us, event | category | flops | bytes accessed | tf_op | source)
XLA Modules:
  0.0 241.0 jit_solution(13976173427043723064)
XLA Ops:
  7.2 0.0 copy-start
  7.2 0.0 all-gather.3.cloned.1.call-start
  7.2 1.2 copy-done
  8.4 0.1 constant_dynamic-slice_fusion.1
  8.5 0.1 copy.46
  8.6 0.7 and_convert_fusion.1
  9.3 0.1 and.45
  9.4 0.1 and.47
  9.5 0.1 shift_right_arithmetic.34
  9.7 20.2 %all_to_all.35 = bf16[8,160,128]{2,1,0:T(8,128)(2,1)S(1)} all-to-all(bf16[8,160,128]{2,1,0:T(8,128)(2,1)S(1)} %broadcast_in_dim.94), channel_id=1, replica_groups=mesh['dp'=8,'vocab'=32] {'dp'}, dimensions={0} | all-to-all | bytes 655360 | tf_op jit(solution)/shard_map/all_to_all | solution.py:19
  29.9 0.7 copy_bitcast_fusion
  30.6 0.0 all-gather.3.cloned.1.call-update
  30.6 4.5 %copy.39 = bf16[2304,576]{1,0:T(8,128)(2,1)} copy(bf16[2304,576]{0,1:T(8,128)(2,1)} %param.10) | data formatting | bytes 5308416 | tf_op args[1]
  35.2 5.9 %all-to-all-start = ((bf16[8,288,576]{2,1,0:T(8,128)(2,1)}), bf16[8,288,576]{2,1,0:T(8,128)(2,1)}, u32[]{:S(2)}, u32[]{:S(2)}) async-start(bf16[8,288,576]{2,1,0:T(8,128)(2,1)} %bitcast.43), calls=%async_computation | async-start | bytes 5898240 | tf_op jit(solution)/shard_map/all_to_all | solution.py:25
  41.1 0.5 broadcast.233
  41.6 0.0 copy-done.5
  41.6 0.7 reduce.16
  42.3 0.1 broadcast_in_dim.59
  42.3 0.0 copy-done.6
  42.3 0.1 add.131
  42.4 0.4 reshape_squeeze.4
  42.8 0.1 select_convert_fusion
  42.9 0.1 pad_maximum_fusion
  43.1 0.6 fusion.51.label_ref
  43.7 64.0 %all-to-all-done.part_ref = bf16[8,288,576]{2,1,0:T(8,128)(2,1)} async-done(((bf16[8,288,576]{2,1,0:T(8,128)(2,1)}), bf16[8,288,576]{2,1,0:T(8,128)(2,1)}, u32[]{:S(2)}, u32[]{:S(2)}) %all-to-all-start) | async-done | bytes 2654240 | tf_op jit(solution)/shard_map/all_to_all | solution.py:25
  107.7 11.1 %forward_block.1 = (bf16[288,1024]{1,0:T(8,128)(2,1)}, f32[2,1024]{1,0:T(2,128)}) custom-call(s32[1]{0:T(128)} %bitcast.first_row_ref, bf16[8,288,576]{2,1,0:T(8,128)(2,1)} %all-to-all-done.part_ref, bf16[4608,1024]{1,0:T(8,128)(2,1)} %all-gather.3.cloned.1.call-done.states_ref, s32[1,1024]{1,0:T(1,128)} %fusion.51.label_ref), custom_call_target="tpu_custom_call" | custom-call | flops 2717908992 | bytes 12091392 | tf_op jit(solution)/shard_map/forward_block/pallas_call | solution.py:80
  118.8 0.0 all-gather.5.cloned.1.call-update
  118.8 0.8 copy.43
  119.7 4.9 %all-to-all-start.5 = ((bf16[8,48,640]{2,1,0:T(8,128)(2,1)}), bf16[8,48,640]{2,1,0:T(8,128)(2,1)S(1)}, u32[]{:S(2)}, u32[]{:S(2)}) async-start(bf16[8,48,640]{2,1,0:T(8,128)(2,1)} %copy.43), calls=%async_computation.5 | async-start | bytes 983040 | tf_op jit(solution)/shard_map/all_to_all | solution.py:25
  124.5 0.3 reduce-window.9
  124.8 0.1 slice.58
  125.0 0.1 add.142
  125.1 0.1 slice_reduce_fusion
  125.2 0.1 iota_compare_fusion.5
  125.2 0.1 add_bitcast_fusion
  125.3 16.7 %all-to-all-done.5 = bf16[8,48,640]{2,1,0:T(8,128)(2,1)S(1)} async-done(((bf16[8,48,640]{2,1,0:T(8,128)(2,1)}), bf16[8,48,640]{2,1,0:T(8,128)(2,1)S(1)}, u32[]{:S(2)}, u32[]{:S(2)}) %all-to-all-start.5) | async-done | bytes 491552 | tf_op jit(solution)/shard_map/all_to_all | solution.py:25
  142.1 0.3 fusion.35
  142.3 0.1 reshape.369
  142.4 0.7 broadcast_in_dim.96
  143.2 7.6 %all-to-all-start.2 = ((f32[32,16,128]{2,1,0:T(8,128)}), f32[32,16,128]{2,1,0:T(8,128)S(1)}, u32[]{:S(2)}, u32[]{:S(2)}) async-start(f32[32,16,128]{2,1,0:T(8,128)} %broadcast_in_dim.96), calls=%async_computation.2 | async-start | bytes 524288 | tf_op jit(solution)/shard_map/all_to_all | solution.py:19
  150.8 0.4 convert_reduce_fusion.1
  151.3 0.1 reduce_sum.45
  151.4 6.4 %all-to-all-done.2 = f32[32,16,128]{2,1,0:T(8,128)S(1)} async-done(((f32[32,16,128]{2,1,0:T(8,128)}), f32[32,16,128]{2,1,0:T(8,128)S(1)}, u32[]{:S(2)}, u32[]{:S(2)}) %all-to-all-start.2) | async-done | bytes 262176 | tf_op jit(solution)/shard_map/all_to_all | solution.py:19
  157.8 0.6 broadcast_in_dim.97
  158.4 5.1 %all-to-all-start.3 = ((f32[8,16,128]{2,1,0:T(8,128)}), f32[8,16,128]{2,1,0:T(8,128)S(1)}, u32[]{:S(2)}, u32[]{:S(2)}) async-start(f32[8,16,128]{2,1,0:T(8,128)} %broadcast_in_dim.97), calls=%async_computation.3 | async-start | bytes 131072 | tf_op jit(solution)/shard_map/all_to_all | solution.py:19
  163.5 2.0 convolution_convert_fusion
  165.5 6.2 %all-to-all-done.3 = f32[8,16,128]{2,1,0:T(8,128)S(1)} async-done(((f32[8,16,128]{2,1,0:T(8,128)}), f32[8,16,128]{2,1,0:T(8,128)S(1)}, u32[]{:S(2)}, u32[]{:S(2)}) %all-to-all-start.3) | async-done | bytes 65568 | tf_op jit(solution)/shard_map/all_to_all | solution.py:19
  171.6 5.9 %all-to-all-start.6 = ((bf16[32,32,640]{2,1,0:T(8,128)(2,1)}), bf16[32,32,640]{2,1,0:T(8,128)(2,1)S(1)}, u32[]{:S(2)}, u32[]{:S(2)}) async-start(bf16[32,32,640]{2,1,0:T(8,128)(2,1)} %bitcast.49), calls=%async_computation.6 | async-start | bytes 2621440 | tf_op jit(solution)/shard_map/all_to_all | solution.py:25
  177.6 3.4 %all-gather.5.cloned.1.call-done = bf16[2304,1024]{1,0:T(8,128)(2,1)} async-done(((bf16[288,1024]{1,0:T(8,128)(2,1)}), bf16[2304,1024]{1,0:T(8,128)(2,1)}) %all-gather.5.cloned.1.call-update) | async-done | bytes 4718608 | tf_op jit(solution)/shard_map/all_gather | solution.py:174
  181.0 6.2 %fusion.5 = bf16[72,8,8,128]{3,1,2,0:T(8,128)(2,1)S(1)} fusion(bf16[2304,576]{0,1:T(8,128)(2,1)} %param.10, bf16[2304,1024]{1,0:T(8,128)(2,1)} %all-gather.5.cloned.1.call-done, s32[1024]{0:T(1024)S(1)} %bitcast.56, s32[2304]{0:T(1024)S(1)} %iota_add_fusion, bf16[1024]{0:T(1024)(128)(2,1)S(1)} %get-tuple-element.33, f32[1024]{0:T(1024)S(1)} %get-tuple-element.32), kind=kOutput, calls=%fused_computation.8 | convolution fusion | flops 2723807232 | bytes 8571904 | tf_op jit(solution)/shard_map/dot_general | solution.py:198
  187.2 0.3 copy.48
  187.5 1.2 copy.42
  188.8 6.8 %all-to-all-done.6 = bf16[32,32,640]{2,1,0:T(8,128)(2,1)S(1)} async-done(((bf16[32,32,640]{2,1,0:T(8,128)(2,1)}), bf16[32,32,640]{2,1,0:T(8,128)(2,1)S(1)}, u32[]{:S(2)}, u32[]{:S(2)}) %all-to-all-start.6) | async-done | bytes 1310752 | tf_op jit(solution)/shard_map/all_to_all | solution.py:25
  195.6 6.4 %all-to-all-start.4 = ((bf16[32,144,128]{2,1,0:T(8,128)(2,1)}), bf16[32,144,128]{2,1,0:T(8,128)(2,1)}, u32[]{:S(2)}, u32[]{:S(2)}) async-start(bf16[32,144,128]{2,1,0:T(8,128)(2,1)} %bitcast.46), calls=%async_computation.4 | async-start | bytes 2359296 | tf_op jit(solution)/shard_map/all_to_all | solution.py:25
  202.0 0.3 add_reduce_fusion
  202.3 0.6 reshape.360
  202.9 6.0 %fusion.23 = f32[256,576]{0,1:T(8,128)} fusion(bf16[4608,1024]{1,0:T(8,128)(2,1)} %all-gather.3.cloned.1.call-done.states_ref, s32[]{:T(128)S(6)} %select_n.36, bf16[2304,1024]{1,0:T(8,128)(2,1)} %all-gather.5.cloned.1.call-done, s32[1024]{0:T(1024)S(1)} %bitcast.57, s32[2304]{0:T(1024)S(1)} %iota_add_fusion, bf16[1024]{0:T(1024)(128)(2,1)S(1)} %get-tuple-element.33, ...), kind=kOutput, calls=%fused_computation.16 | convolution fusion | flops 1516371968 | bytes 6519044 | tf_op jit(solution)/shard_map/dot_general | solution.py:228
  208.9 2.9 %multiply_add_fusion = (f32[256,576]{0,1:T(8,128)}, f32[256,576]{0,1:T(8,128)}) fusion(f32[256,576]{0,1:T(8,128)S(1)} %copy-done.1, f32[256,576]{0,1:T(8,128)} %param.17, f32[256,576]{0,1:T(8,128)} %fusion.23, bf16[1024,640]{1,0:T(8,128)(2,1)S(1)} %bitcast.45, s32[1024]{0:T(1024)S(1)} %add_reduce_fusion), kind=kOutput, calls=%fused_computation.26 | convolution fusion | flops 303431680 | bytes 4263936 | tf_op jit(solution)/shard_map/dot_general | solution.py:234
  211.8 6.7 %all-to-all-done.4 = bf16[32,144,128]{2,1,0:T(8,128)(2,1)} async-done(((bf16[32,144,128]{2,1,0:T(8,128)(2,1)}), bf16[32,144,128]{2,1,0:T(8,128)(2,1)}, u32[]{:S(2)}, u32[]{:S(2)}) %all-to-all-start.4) | async-done | bytes 1179680 | tf_op jit(solution)/shard_map/all_to_all | solution.py:25
  218.6 1.4 reduce_sum.43
  220.0 5.7 %collective-permute-start = (bf16[144,128]{1,0:T(8,128)(2,1)S(1)}, bf16[144,128]{1,0:T(8,128)(2,1)S(1)}, u32[]{:S(2)}, u32[]{:S(2)}) collective-permute-start(bf16[144,128]{1,0:T(8,128)(2,1)S(1)} %reduce_sum.43), channel_id=1, source_target_pairs={{0,0},{1,1},{2,2},{3,3},{4,32},{5,33},{6,34},{7,35},{8,64},{9,65},... | collective-permute-start | bytes 110600 | tf_op jit(solution)/shard_map/ppermute | solution.py:210
  225.7 3.9 %fusion.20 = f32[256,576]{0,1:T(8,128)} fusion(bf16[2304,576]{0,1:T(8,128)(2,1)} %param.10, s32[2304]{0:T(1024)S(1)} %add_bitcast_fusion, pred[2304]{0:T(1024)(128)(4,1)S(1)} %broadcast_compare_fusion, f32[256,576]{0,1:T(8,128)} %get-tuple-element.31, f32[256,576]{0,1:T(8,128)} %get-tuple-element.30), kind=kOutput, calls=%fused_computation.15 | convolution fusion | flops 681541632 | bytes 4435200 | tf_op jit(solution)/shard_map/dot_general | solution.py:223
  229.6 3.8 %collective-permute-done = bf16[144,128]{1,0:T(8,128)(2,1)S(1)} collective-permute-done((bf16[144,128]{1,0:T(8,128)(2,1)S(1)}, bf16[144,128]{1,0:T(8,128)(2,1)S(1)}, u32[]{:S(2)}, u32[]{:S(2)}) %collective-permute-start) | collective-permute-done | bytes 36896 | tf_op jit(solution)/shard_map/ppermute | solution.py:210
  233.4 0.7 copy.45
  (31 shorter events, 0.3 us)
Async XLA Ops:
  7.2 1.3 copy-start
  7.2 100.5 %all-gather.3.cloned.1.call-start = ((), (), s32[]{:S(2)}) async-start(), calls=%async_computation.7 | async-start | bytes 9732096 | tf_op jit(solution)/shard_map/all_gather | solution.py:153
  35.2 6.4 %copy-start.5 = (s32[1,2,24,1]{2,3,1,0:T(1,128)S(1)}, s32[1,2,24,1]{2,3,1,0:T(1,128)}, u32[]{:S(2)}) copy-start(s32[1,2,24,1]{2,3,1,0:T(1,128)} %param.14) | copy-start | bytes 580
  35.2 7.2 %copy-start.6 = (s32[1,2,24]{2,1,0:T(2,128)S(1)}, s32[1,2,24]{2,1,0:T(2,128)}, u32[]{:S(2)}) copy-start(s32[1,2,24]{2,1,0:T(2,128)} %param.15) | copy-start | bytes 580
  35.2 7.3 %copy-start.2 = (bf16[1,2,24,4608]{3,2,1,0:T(8,128)(2,1)S(1)}, bf16[1,2,24,4608]{3,2,1,0:T(8,128)(2,1)}, u32[]{:S(2)}) copy-start(bf16[1,2,24,4608]{3,2,1,0:T(8,128)(2,1)} %param.13) | copy-start | bytes 1327108
  35.2 72.5 %all-to-all-start = ((bf16[8,288,576]{2,1,0:T(8,128)(2,1)}), bf16[8,288,576]{2,1,0:T(8,128)(2,1)}, u32[]{:S(2)}, u32[]{:S(2)}) async-start(bf16[8,288,576]{2,1,0:T(8,128)(2,1)} %bitcast.43), calls=%async_computation | async-start | bytes 5898240 | tf_op jit(solution)/shard_map/all_to_all | solution.py:25
  41.1 139.9 %all-gather.5.cloned.1.call-start = ((), (), s32[]{:S(2)}) async-start(), calls=%async_computation.8 | async-start | bytes 5308416 | tf_op jit(solution)/shard_map/all_gather | solution.py:174
  107.7 16.9 %copy-start.3 = (s32[2304]{0:T(1024)S(1)}, s32[2304]{0:T(1024)}, u32[]{:S(2)}) copy-start(s32[2304]{0:T(1024)} %param.11) | copy-start | bytes 27652
  118.8 23.6 %copy-start.4 = (f32[2,1024]{1,0:T(2,128)S(1)}, f32[2,1024]{1,0:T(2,128)}, u32[]{:S(2)}) copy-start(f32[2,1024]{1,0:T(2,128)} %get-tuple-element.10) | copy-start | bytes 24580
  119.7 22.4 %all-to-all-start.5 = ((bf16[8,48,640]{2,1,0:T(8,128)(2,1)}), bf16[8,48,640]{2,1,0:T(8,128)(2,1)S(1)}, u32[]{:S(2)}, u32[]{:S(2)}) async-start(bf16[8,48,640]{2,1,0:T(8,128)(2,1)} %copy.43), calls=%async_computation.5 | async-start | bytes 983040 | tf_op jit(solution)/shard_map/all_to_all | solution.py:25
  143.2 14.6 %all-to-all-start.2 = ((f32[32,16,128]{2,1,0:T(8,128)}), f32[32,16,128]{2,1,0:T(8,128)S(1)}, u32[]{:S(2)}, u32[]{:S(2)}) async-start(f32[32,16,128]{2,1,0:T(8,128)} %broadcast_in_dim.96), calls=%async_computation.2 | async-start | bytes 524288 | tf_op jit(solution)/shard_map/all_to_all | solution.py:19
  158.4 13.2 %all-to-all-start.3 = ((f32[8,16,128]{2,1,0:T(8,128)}), f32[8,16,128]{2,1,0:T(8,128)S(1)}, u32[]{:S(2)}, u32[]{:S(2)}) async-start(f32[8,16,128]{2,1,0:T(8,128)} %broadcast_in_dim.97), calls=%async_computation.3 | async-start | bytes 131072 | tf_op jit(solution)/shard_map/all_to_all | solution.py:19
  171.6 23.9 %all-to-all-start.6 = ((bf16[32,32,640]{2,1,0:T(8,128)(2,1)}), bf16[32,32,640]{2,1,0:T(8,128)(2,1)S(1)}, u32[]{:S(2)}, u32[]{:S(2)}) async-start(bf16[32,32,640]{2,1,0:T(8,128)(2,1)} %bitcast.49), calls=%async_computation.6 | async-start | bytes 2621440 | tf_op jit(solution)/shard_map/all_to_all | solution.py:25
  195.6 23.0 %all-to-all-start.4 = ((bf16[32,144,128]{2,1,0:T(8,128)(2,1)}), bf16[32,144,128]{2,1,0:T(8,128)(2,1)}, u32[]{:S(2)}, u32[]{:S(2)}) async-start(bf16[32,144,128]{2,1,0:T(8,128)(2,1)} %bitcast.46), calls=%async_computation.4 | async-start | bytes 2359296 | tf_op jit(solution)/shard_map/all_to_all | solution.py:25
  202.9 6.0 %copy-start.1 = (f32[256,576]{0,1:T(8,128)S(1)}, f32[256,576]{0,1:T(8,128)}, u32[]{:S(2)}) copy-start(f32[256,576]{0,1:T(8,128)} %param.16) | copy-start | bytes 1769476
  220.0 13.4 %collective-permute-start = (bf16[144,128]{1,0:T(8,128)(2,1)S(1)}, bf16[144,128]{1,0:T(8,128)(2,1)S(1)}, u32[]{:S(2)}, u32[]{:S(2)}) collective-permute-start(bf16[144,128]{1,0:T(8,128)(2,1)S(1)} %reduce_sum.43), channel_id=1, source_target_pairs={{0,0},{1,1},{2,2},{3,3},{4,32},{5,33},{6,34},{7,35},{8,64},{9,65},... | collective-permute-start | bytes 110600 | tf_op jit(solution)/shard_map/ppermute | solution.py:210
Sparse Core Ops, SparseCore 0:
  30.8 57.3 all-gather.2
  119.0 62.0 all-gather.4
where the time goes:
time: 242 us; the launch traced here: 241 us
  waiting for transfers between devices  114 us (47%)
  starting transfers between devices  41.5 us (17%)
  matrix products  20.9 us (9%)
  blocking collectives  20.2 us (8%)
  between operations  14.3 us (6%)
  local copies, waits for them, and re-layouts  13.7 us (6%)
  Pallas kernels  11.1 us (5%)
  other arithmetic  5.19 us (2%)
    all_to_all x4, waiting for transfers between devices, exchanged(): return lax.all_to_all(parts, axis, split_axis=0, concat_axis=0, tiled=True)  94.3 us
    all_to_all x4, starting transfers between devices, exchanged(): return lax.all_to_all(parts, axis, split_axis=0, concat_axis=0, tiled=True)  23.1 us
    all_to_all x1, blocking collectives, sent_to_all(): lax.all_to_all(jnp.broadcast_to(array[None], (peers, *array.shape)), axis...  20.2 us
    all_to_all x2, starting transfers between devices, sent_to_all(): lax.all_to_all(jnp.broadcast_to(array[None], (peers, *array.shape)), axis...  12.7 us
    all_to_all x2, waiting for transfers between devices, sent_to_all(): lax.all_to_all(jnp.broadcast_to(array[None], (peers, *array.shape)), axis...  12.6 us
    pallas_call x1, Pallas kernels, forward_block(): pl.pallas_call(forward_kernel, grid=(parts,), in_specs=[pl.BlockSpec(memo...  11.1 us
    unnamed x19, local copies, waits for them, and re-layouts  7.43 us
    dot_general x1, matrix products, body(): lax.dot_general(table, error, (((0,), (0,)), ((), ())), preferred_element...  6.18 us
  transfers between devices with their start and end apart: 9, of which 8 were waited for; matrix products, arithmetic and copies ran while one was open for 14% of the time, Pallas kernels for 0%

commit v1 on v0

--- a/solution.py
+++ b/solution.py
@@ -34,9 +34,24 @@
     return low + (middle << 8) + (high << 16)
 
 
-def forward_kernel(first_row_ref, part_ref, states_ref, label_ref, weight_ref, sums_ref, raw_ref):
+def forward_kernel(place_ref, *refs):
+    part_refs = refs[:-6]
+    states_ref, label_ref, weight_ref, sums_ref, raw_ref, part_ref = refs[-6:]
     step = pl.program_id(0)
-    product = jnp.dot(part_ref[0], states_ref[...], preferred_element_type=jnp.float32)
+    rows, columns = part_ref.shape
+    whole = columns // 128
+
+    for k, packed_ref in enumerate(part_refs):
+
+        @pl.when(step == k)
+        def _(packed_ref=packed_ref):
+            for at in range(whole):
+                part_ref[:, at * 128 : (at + 1) * 128] = packed_ref[at * rows : (at + 1) * rows, :]
+            rest = packed_ref[whole * rows :, :]
+            part_ref[: rows // 2, whole * 128 :] = rest[:, :64]
+            part_ref[rows // 2 :, whole * 128 :] = rest[:, 64:]
+
+    product = jnp.dot(part_ref[...], states_ref[...], preferred_element_type=jnp.float32)
 
     @pl.when(step == 0)
     def _():
@@ -48,7 +63,7 @@
 
     @pl.when(step == pl.num_programs(0) - 1)
     def _():
-        rows, tokens = raw_ref.shape
+        tokens = raw_ref.shape[1]
         strip = 16
         labels = label_ref[...]
 
@@ -59,7 +74,7 @@
             capped = cap_value * squashed
             expd = jnp.exp(capped)
             ids = (
-                lax.broadcasted_iota(jnp.int32, (strip, tokens), 0) + first_row_ref[0] + k * strip
+                lax.broadcasted_iota(jnp.int32, (strip, tokens), 0) + place_ref[0] + k * strip
             )
             weight_ref[at, :] = (expd * (1.0 - squashed * squashed)).astype(weight_ref.dtype)
             picked = jnp.where(ids == labels, capped, 0.0)
@@ -74,27 +89,33 @@
         sums_ref[1:2, :] = jnp.sum(pick, axis=0, keepdims=True)
 
 
-def forward_block(whole, states, label_row, first_row):
-    parts, rows, columns = whole.shape
+def forward_block(whole, states, label_row, first_row, group, columns):
+    parts = len(whole)
+    rows = whole[0].size // columns
     tokens = states.shape[1]
     return pl.pallas_call(
         forward_kernel,
-        grid=(parts,),
-        in_specs=[
-            pl.BlockSpec(memory_space=pltpu.SMEM),
-            pl.BlockSpec((1, rows, columns), lambda k: (k, 0, 0)),
-            pl.BlockSpec((columns, tokens), lambda k: (k, 0)),
-            pl.BlockSpec((1, tokens), lambda k: (0, 0)),
-        ],
-        out_specs=[
-            pl.BlockSpec((rows, tokens), lambda k: (0, 0)),
-            pl.BlockSpec((2, tokens), lambda k: (0, 0)),
-        ],
+        grid_spec=pltpu.PrefetchScalarGridSpec(
+            num_scalar_prefetch=1,
+            grid=(parts,),
+            in_specs=[
+                *[pl.BlockSpec(part.shape, lambda k, place: (0, 0)) for part in whole],
+                pl.BlockSpec((columns, tokens), lambda k, place: ((place[1] - k) & (parts - 1), 0)),
+                pl.BlockSpec((1, tokens), lambda k, place: (0, 0)),
+            ],
+            out_specs=[
+                pl.BlockSpec((rows, tokens), lambda k, place: (0, 0)),
+                pl.BlockSpec((2, tokens), lambda k, place: (0, 0)),
+            ],
+            scratch_shapes=[
+                pltpu.VMEM((rows, tokens), jnp.float32),
+                pltpu.VMEM((rows, columns), jnp.bfloat16),
+            ],
+        ),
         out_shape=[
             jax.ShapeDtypeStruct((rows, tokens), jnp.bfloat16),
             jax.ShapeDtypeStruct((2, tokens), jnp.float32),
         ],
-        scratch_shapes=[pltpu.VMEM((rows, tokens), jnp.float32)],
         compiler_params=pltpu.CompilerParams(dimension_semantics=("arbitrary",)),
         cost_estimate=pl.CostEstimate(
             flops=2 * parts * rows * columns * tokens,
@@ -102,7 +123,62 @@
             transcendentals=2 * rows * tokens,
         ),
         name="forward_block",
-    )(first_row.reshape(1), whole, states, label_row.reshape(1, tokens))
+    )(jnp.stack([first_row, group]), *whole, states, label_row.reshape(1, tokens))
+
+
+def spread(parts, axis):
+    peers = len(parts)
+    middle = peers // 2
+    order = sorted(range(1, peers), key=lambda away: (abs(away - middle), away))
+    came = {0: parts[0]}
+    for away in order:
+        came[away] = lax.ppermute(
+            parts[away], axis, [(k, (k + away) % peers) for k in range(peers)]
+        )
+    return [came[k] for k in range(peers)]
+
+
+def packing_kernel(group_ref, table_ref, *refs):
+    part_refs, rows_ref = refs[:-1], refs[-1]
+    columns, rows = table_ref.shape
+    lanes = 128
+    peers = len(part_refs)
+    part = rows // peers
+    whole = columns // lanes
+    for at in range(0, rows, lanes):
+        rows_ref[at : at + lanes, :] = table_ref[:, at : at + lanes].T
+    for away in range(peers):
+        first = pl.multiple_of(((group_ref[0] + away) & (peers - 1)) * part, part)
+        for k in range(whole):
+            part_refs[away][k * part : (k + 1) * part, :] = rows_ref[
+                pl.ds(first, part), k * lanes : (k + 1) * lanes
+            ]
+        part_refs[away][whole * part :, :] = jnp.concatenate(
+            [
+                rows_ref[pl.ds(first, part // 2), whole * lanes :],
+                rows_ref[pl.ds(first + part // 2, part // 2), whole * lanes :],
+            ],
+            axis=1,
+        )
+
+
+def packed_parts(table, group, peers):
+    rows, columns = table.shape
+    part = jax.ShapeDtypeStruct((rows * columns // peers // 128, 128), table.dtype)
+    return pl.pallas_call(
+        packing_kernel,
+        in_specs=[
+            pl.BlockSpec(memory_space=pltpu.SMEM),
+            pl.BlockSpec(memory_space=pltpu.VMEM),
+        ],
+        out_specs=[pl.BlockSpec(memory_space=pltpu.VMEM)] * peers,
+        out_shape=[part] * peers,
+        scratch_shapes=[pltpu.VMEM((rows, columns), table.dtype)],
+        cost_estimate=pl.CostEstimate(
+            flops=rows * columns * 8, bytes_accessed=rows * columns * 4, transcendentals=0
+        ),
+        name="packed_parts",
+    )(group.reshape(1), table.T)
 
 
 def select_rows(new_mask, new_count):
@@ -153,7 +229,8 @@
     states = lax.all_gather(slices, "vocab", axis=0, tiled=True)
     label_row = from_digits(arrived[:, piece : piece + 3].transpose(1, 0, 2)).reshape(total_tokens)
 
-    whole = exchanged(table.reshape(groups, row_part, columns), "dp")
+    prepared = packed_parts(table, group, groups)
+    whole = spread(prepared, "dp")
 
     items = blocks * items_here
     item_columns = in_grad[0].reshape(items, groups, columns).transpose(1, 0, 2)
@@ -166,10 +243,10 @@
     item_columns = jnp.concatenate(
         [item_columns, jnp.broadcast_to(marks[None], (groups, items, 64))], axis=2
     )
-    whole, item_columns = lax.optimization_barrier((whole, item_columns))
+    item_columns = exchanged(item_columns, "dp")
 
     weights, local_sums = forward_block(
-        whole, states, label_row, shard * rows + group * row_part
+        whole, states, label_row, shard * rows + group * row_part, group, columns
     )
     all_weights = lax.all_gather(weights, "dp", axis=0, tiled=True)
 
@@ -180,7 +257,6 @@
     loss = lax.dynamic_slice(
         (jnp.log(total) - picked).reshape(groups, tokens), (group, 0), (1, tokens)
     )
-    item_columns = exchanged(item_columns, "dp")
     sent_rows = pack_items(item_columns, columns, groups * blocks, shards, capacity)
     got_rows = exchanged(sent_rows, "vocab").reshape(-1, columns + 64)
     targets = got_rows[:, columns + 1].astype(jnp.int32) - 1

time: 242 us -> 240 us (level)
  waiting for transfers between devices: 114 us -> 99.7 us
  starting transfers between devices: 41.5 us -> 52 us
  Pallas kernels: 11.1 us -> 17.2 us
  local copies, waits for them, and re-layouts: 13.7 us -> 9.22 us
    all_to_all x4 -> x3, waiting for transfers between devices: 94.3 us -> 33 us  [exchanged(): return lax.all_to_all(parts, axis, split_axis=0, concat_axis=0, tiled=True)]
    ppermute x0 -> x7, waiting for transfers between devices: none -> 47.3 us  [spread(): lax.ppermute(parts[away], axis, [(k, (k + away) % peers) for k in range(p...]
    ppermute x0 -> x7, starting transfers between devices: none -> 15.4 us  [spread(): lax.ppermute(parts[away], axis, [(k, (k + away) % peers) for k in range(p...]
    pallas_call x1 -> x2, Pallas kernels: 11.1 us -> 17.2 us  [the longest x1 12.7 us: forward_block(): pl.pallas_call(forward_kernel, grid_spec=pltpu.PrefetchScalarGridSpec(num...]
    all_to_all x4 -> x3, starting transfers between devices: 23.1 us -> 17.9 us  [exchanged(): return lax.all_to_all(parts, axis, split_axis=0, concat_axis=0, tiled=True)]
    unnamed x19 -> x28, local copies, waits for them, and re-layouts: 7.43 us -> 2.94 us
  transfers between devices with their start and end apart: 9 -> 15, of which waited for: 8 -> 12; matrix products, arithmetic and copies ran while one was open for 14% -> 13% of each run, Pallas kernels for 0% -> 2%
where the time goes in v1:
time: 240 us; the launch traced here: 239 us
  waiting for transfers between devices  99.7 us (42%)
  starting transfers between devices  52 us (22%)
  matrix products  20.9 us (9%)
  blocking collectives  20.2 us (8%)
  Pallas kernels  17.2 us (7%)
  between operations  14.3 us (6%)
  local copies, waits for them, and re-layouts  9.22 us (4%)
  other arithmetic  5.92 us (2%)
    ppermute x7, waiting for transfers between devices, spread(): lax.ppermute(parts[away], axis, [(k, (k + away) % peers) for k in range(p...  47.3 us
    all_to_all x3, waiting for transfers between devices, exchanged(): return lax.all_to_all(parts, axis, split_axis=0, concat_axis=0, tiled=True)  33 us
    all_to_all x1, blocking collectives, sent_to_all(): lax.all_to_all(jnp.broadcast_to(array[None], (peers, *array.shape)), axis...  20.2 us
    all_to_all x3, starting transfers between devices, exchanged(): return lax.all_to_all(parts, axis, split_axis=0, concat_axis=0, tiled=True)  17.9 us
    ppermute x7, starting transfers between devices, spread(): lax.ppermute(parts[away], axis, [(k, (k + away) % peers) for k in range(p...  15.4 us
    all_to_all x2, starting transfers between devices, sent_to_all(): lax.all_to_all(jnp.broadcast_to(array[None], (peers, *array.shape)), axis...  13 us
    pallas_call x1, Pallas kernels, forward_block(): pl.pallas_call(forward_kernel, grid_spec=pltpu.PrefetchScalarGridSpec(num...  12.7 us
    all_to_all x2, waiting for transfers between devices, sent_to_all(): lax.all_to_all(jnp.broadcast_to(array[None], (peers, *array.shape)), axis...  12.6 us
  transfers between devices with their start and end apart: 15, of which 12 were waited for; matrix products, arithmetic and copies ran while one was open for 13% of the time, Pallas kernels for 2%

profile of v1, /device:TPU:38, one launch (start us, length us, event | category | flops | bytes accessed | tf_op | source)
XLA Modules:
  0.0 239.5 jit_solution(3099374218005474320)
XLA Ops:
  7.2 1.2 copy-done
  8.4 0.1 constant_dynamic-slice_fusion.1
  8.5 0.1 copy.40
  8.6 0.7 and_convert_fusion.1
  9.3 0.1 and.45
  9.4 0.1 and.47
  9.5 0.1 shift_right_arithmetic.34
  9.7 20.2 %all_to_all.30 = bf16[8,160,128]{2,1,0:T(8,128)(2,1)S(1)} all-to-all(bf16[8,160,128]{2,1,0:T(8,128)(2,1)S(1)} %broadcast_in_dim.58), channel_id=1, replica_groups=mesh['dp'=8,'vocab'=32] {'dp'}, dimensions={0} | all-to-all | bytes 655360 | tf_op jit(solution)/shard_map/all_to_all | solution.py:19
  29.9 0.8 copy_bitcast_fusion
  30.7 4.6 %packed_parts.1 = (bf16[1296,128]{1,0:T(8,128)(2,1)}, bf16[1296,128]{1,0:T(8,128)(2,1)}, bf16[1296,128]{1,0:T(8,128)(2,1)}, bf16[1296,128]{1,0:T(8,128)(2,1)}, b...) custom-call(s32[1]{0:T(128)} %bitcast.1.group_ref, ...), custom_call_target="tpu_custom_call" | custom-call | flops 10616832 | bytes 5308416 | tf_op jit(solution)/shard_map/packed_parts/pallas_call | solution.py:168
  35.3 0.5 collective-permute-start
  35.7 0.7 collective-permute-start.1
  36.4 2.7 %collective-permute-start.2 = (bf16[1296,128]{1,0:T(8,128)(2,1)}, bf16[1296,128]{1,0:T(8,128)(2,1)S(1)}, u32[]{:S(2)}, u32[]{:S(2)}) collective-permute-start(bf16[1296,128]{1,0:T(8,128)(2,1)} %get-tuple-element.18), channel_id=1, source_target_pairs={{0,96},{32,128},{64,160},{96,192},{128,224},{160,0},{192,32},{224,... | collective-permute-start | bytes 995336 | tf_op jit(solution)/shard_map/ppermute | solution.py:135
  39.1 3.0 %collective-permute-start.3 = (bf16[1296,128]{1,0:T(8,128)(2,1)}, bf16[1296,128]{1,0:T(8,128)(2,1)S(1)}, u32[]{:S(2)}, u32[]{:S(2)}) collective-permute-start(bf16[1296,128]{1,0:T(8,128)(2,1)} %get-tuple-element.19), channel_id=1, source_target_pairs={{0,128},{32,160},{64,192},{96,224},{128,0},{160,32},{192,64},{224,... | collective-permute-start | bytes 995336 | tf_op jit(solution)/shard_map/ppermute | solution.py:135
  42.1 4.6 %collective-permute-start.4 = (bf16[1296,128]{1,0:T(8,128)(2,1)}, bf16[1296,128]{1,0:T(8,128)(2,1)S(1)}, u32[]{:S(2)}, u32[]{:S(2)}) collective-permute-start(bf16[1296,128]{1,0:T(8,128)(2,1)} %get-tuple-element.20), channel_id=1, source_target_pairs={{0,160},{32,192},{64,224},{96,0},{128,32},{160,64},{192,96},{224,1... | collective-permute-start | bytes 995336 | tf_op jit(solution)/shard_map/ppermute | solution.py:135
  46.8 0.7 pad_add_fusion.place_ref
  47.5 2.9 %collective-permute-done.refs_1_ = bf16[1296,128]{1,0:T(8,128)(2,1)S(1)} collective-permute-done((bf16[1296,128]{1,0:T(8,128)(2,1)}, bf16[1296,128]{1,0:T(8,128)(2,1)S(1)}, u32[]{:S(2)}, u32[]{:S(2)}) %collective-permute-start) | collective-permute-done | bytes 331808 | tf_op jit(solution)/shard_map/ppermute | solution.py:135
  50.4 3.9 %collective-permute-start.5 = (bf16[1296,128]{1,0:T(8,128)(2,1)}, bf16[1296,128]{1,0:T(8,128)(2,1)}, u32[]{:S(2)}, u32[]{:S(2)}) collective-permute-start(bf16[1296,128]{1,0:T(8,128)(2,1)} %get-tuple-element.21), channel_id=1, source_target_pairs={{0,192},{32,224},{64,0},{96,32},{128,64},{160,96},{192,128},{224,1... | collective-permute-start | bytes 995336 | tf_op jit(solution)/shard_map/ppermute | solution.py:135
  54.3 13.1 %collective-permute-done.1.refs_2_ = bf16[1296,128]{1,0:T(8,128)(2,1)S(1)} collective-permute-done((bf16[1296,128]{1,0:T(8,128)(2,1)}, bf16[1296,128]{1,0:T(8,128)(2,1)S(1)}, u32[]{:S(2)}, u32[]{:S(2)}) %collective-permute-start.1) | collective-permute-done | bytes 331808 | tf_op jit(solution)/shard_map/ppermute | solution.py:135
  67.4 0.7 fusion.51.refs_9_
  68.1 16.8 %collective-permute-done.2.refs_3_ = bf16[1296,128]{1,0:T(8,128)(2,1)S(1)} collective-permute-done((bf16[1296,128]{1,0:T(8,128)(2,1)}, bf16[1296,128]{1,0:T(8,128)(2,1)S(1)}, u32[]{:S(2)}, u32[]{:S(2)}) %collective-permute-start.2) | collective-permute-done | bytes 331808 | tf_op jit(solution)/shard_map/ppermute | solution.py:135
  84.9 8.9 %collective-permute-done.5.refs_6_ = bf16[1296,128]{1,0:T(8,128)(2,1)} collective-permute-done((bf16[1296,128]{1,0:T(8,128)(2,1)}, bf16[1296,128]{1,0:T(8,128)(2,1)}, u32[]{:S(2)}, u32[]{:S(2)}) %collective-permute-start.5) | collective-permute-done | bytes 331808 | tf_op jit(solution)/shard_map/ppermute | solution.py:135
  93.9 5.5 %collective-permute-done.6.refs_7_ = bf16[1296,128]{1,0:T(8,128)(2,1)} collective-permute-done((bf16[1296,128]{1,0:T(8,128)(2,1)}, bf16[1296,128]{1,0:T(8,128)(2,1)}, u32[]{:S(2)}, u32[]{:S(2)}) %collective-permute-start.6) | collective-permute-done | bytes 331808 | tf_op jit(solution)/shard_map/ppermute | solution.py:135
  99.4 12.7 %forward_block.1 = (bf16[288,1024]{1,0:T(8,128)(2,1)}, f32[2,1024]{1,0:T(2,128)}) custom-call(s32[2]{0:T(128)} %pad_add_fusion.place_ref, bf16[1296,128]{1,0:T(8,128)(2,1)} %get-tuple-element.15.refs_0_, bf16[1296,128]{1,0:T(8,128)(2,1)} %copy-done.3, bf16[1296,128]{1,0:T(8,128)(2,1)} %copy-done.4, bf16[1296,128]{1,0:T(8,128)(2,1)} %copy-done.5, ...), custom_call_target="tpu_custom_call" | custom-call | flops 2717908992 | bytes 12091392 | tf_op jit(solution)/shard_map/forward_block/pallas_call | solution.py:96
  112.1 0.5 broadcast.233
  112.6 0.7 reduce.16
  113.3 0.1 broadcast_in_dim.93
  113.4 0.1 add.140
  113.5 0.4 reshape_squeeze.10
  114.0 0.1 pad_maximum_fusion
  114.1 0.8 copy.37
  114.9 5.4 %all-to-all-start.4 = ((bf16[8,48,640]{2,1,0:T(8,128)(2,1)}), bf16[8,48,640]{2,1,0:T(8,128)(2,1)S(1)}, u32[]{:S(2)}, u32[]{:S(2)}) async-start(bf16[8,48,640]{2,1,0:T(8,128)(2,1)} %copy.37), calls=%async_computation.4 | async-start | bytes 983040 | tf_op jit(solution)/shard_map/all_to_all | solution.py:25
  120.4 0.3 reduce-window.9
  120.8 0.1 add.142
  120.9 0.1 slice_reduce_fusion
  121.2 19.0 %all-to-all-done.4 = bf16[8,48,640]{2,1,0:T(8,128)(2,1)S(1)} async-done(((bf16[8,48,640]{2,1,0:T(8,128)(2,1)}), bf16[8,48,640]{2,1,0:T(8,128)(2,1)S(1)}, u32[]{:S(2)}, u32[]{:S(2)}) %all-to-all-start.4) | async-done | bytes 491552 | tf_op jit(solution)/shard_map/all_to_all | solution.py:25
  140.1 0.3 fusion.35
  140.4 0.1 reshape.362
  140.5 0.7 broadcast_in_dim.60
  141.2 7.7 %all-to-all-start.1 = ((f32[32,16,128]{2,1,0:T(8,128)}), f32[32,16,128]{2,1,0:T(8,128)S(1)}, u32[]{:S(2)}, u32[]{:S(2)}) async-start(f32[32,16,128]{2,1,0:T(8,128)} %broadcast_in_dim.60), calls=%async_computation.1 | async-start | bytes 524288 | tf_op jit(solution)/shard_map/all_to_all | solution.py:19
  149.0 0.4 convert_reduce_fusion.1
  149.4 0.1 reduce_sum.45
  149.5 6.4 %all-to-all-done.1 = f32[32,16,128]{2,1,0:T(8,128)S(1)} async-done(((f32[32,16,128]{2,1,0:T(8,128)}), f32[32,16,128]{2,1,0:T(8,128)S(1)}, u32[]{:S(2)}, u32[]{:S(2)}) %all-to-all-start.1) | async-done | bytes 262176 | tf_op jit(solution)/shard_map/all_to_all | solution.py:19
  156.0 0.6 broadcast_in_dim.61
  156.6 5.2 %all-to-all-start.2 = ((f32[8,16,128]{2,1,0:T(8,128)}), f32[8,16,128]{2,1,0:T(8,128)S(1)}, u32[]{:S(2)}, u32[]{:S(2)}) async-start(f32[8,16,128]{2,1,0:T(8,128)} %broadcast_in_dim.61), calls=%async_computation.2 | async-start | bytes 131072 | tf_op jit(solution)/shard_map/all_to_all | solution.py:19
  161.8 1.9 convolution_convert_fusion
  163.8 6.2 %all-to-all-done.2 = f32[8,16,128]{2,1,0:T(8,128)S(1)} async-done(((f32[8,16,128]{2,1,0:T(8,128)}), f32[8,16,128]{2,1,0:T(8,128)S(1)}, u32[]{:S(2)}, u32[]{:S(2)}) %all-to-all-start.2) | async-done | bytes 65568 | tf_op jit(solution)/shard_map/all_to_all | solution.py:19
  170.0 6.1 %all-to-all-start.5 = ((bf16[32,32,640]{2,1,0:T(8,128)(2,1)}), bf16[32,32,640]{2,1,0:T(8,128)(2,1)S(1)}, u32[]{:S(2)}, u32[]{:S(2)}) async-start(bf16[32,32,640]{2,1,0:T(8,128)(2,1)} %bitcast.50), calls=%async_computation.5 | async-start | bytes 2621440 | tf_op jit(solution)/shard_map/all_to_all | solution.py:25
  176.1 3.0 %all-gather.5.cloned.1.call-done = bf16[2304,1024]{1,0:T(8,128)(2,1)} async-done(((bf16[288,1024]{1,0:T(8,128)(2,1)}), bf16[2304,1024]{1,0:T(8,128)(2,1)}) %all-gather.5.cloned.1.call-update) | async-done | bytes 4718608 | tf_op jit(solution)/shard_map/all_gather | solution.py:251
  179.1 6.2 %fusion.5 = bf16[72,8,8,128]{3,1,2,0:T(8,128)(2,1)S(1)} fusion(bf16[2304,576]{0,1:T(8,128)(2,1)} %param.10, bf16[2304,1024]{1,0:T(8,128)(2,1)} %all-gather.5.cloned.1.call-done, s32[1024]{0:T(1024)S(1)} %bitcast.57, s32[2304]{0:T(1024)S(1)} %iota_add_fusion, bf16[1024]{0:T(1024)(128)(2,1)S(1)} %get-tuple-element.45, f32[1024]{0:T(1024)S(1)} %get-tuple-element.44), kind=kOutput, calls=%fused_computation.8 | convolution fusion | flops 2723807232 | bytes 8571904 | tf_op jit(solution)/shard_map/dot_general | solution.py:274
  185.3 0.3 copy.42
  185.6 1.2 copy.36
  186.8 7.2 %all-to-all-done.5 = bf16[32,32,640]{2,1,0:T(8,128)(2,1)S(1)} async-done(((bf16[32,32,640]{2,1,0:T(8,128)(2,1)}), bf16[32,32,640]{2,1,0:T(8,128)(2,1)S(1)}, u32[]{:S(2)}, u32[]{:S(2)}) %all-to-all-start.5) | async-done | bytes 1310752 | tf_op jit(solution)/shard_map/all_to_all | solution.py:25
  194.1 6.3 %all-to-all-start.3 = ((bf16[32,144,128]{2,1,0:T(8,128)(2,1)}), bf16[32,144,128]{2,1,0:T(8,128)(2,1)}, u32[]{:S(2)}, u32[]{:S(2)}) async-start(bf16[32,144,128]{2,1,0:T(8,128)(2,1)} %bitcast.46), calls=%async_computation.3 | async-start | bytes 2359296 | tf_op jit(solution)/shard_map/all_to_all | solution.py:25
  200.4 0.3 add_reduce_fusion
  200.8 0.6 reshape.353
  201.4 6.0 %fusion.23 = f32[256,576]{0,1:T(8,128)} fusion(bf16[4608,1024]{1,0:T(8,128)(2,1)} %all-gather.3.cloned.1.call-done.refs_8_, s32[]{:T(128)S(6)} %select_n.34, bf16[2304,1024]{1,0:T(8,128)(2,1)} %all-gather.5.cloned.1.call-done, s32[1024]{0:T(1024)S(1)} %bitcast.58, s32[2304]{0:T(1024)S(1)} %iota_add_fusion, bf16[1024]{0:T(1024)(128)(2,1)S(1)} %get-tuple-element.45, ...), kind=kOutput, calls=%fused_computation.16 | convolution fusion | flops 1516371968 | bytes 6519044 | tf_op jit(solution)/shard_map/dot_general | solution.py:304
  207.4 2.9 %multiply_add_fusion = (f32[256,576]{0,1:T(8,128)}, f32[256,576]{0,1:T(8,128)}) fusion(f32[256,576]{0,1:T(8,128)S(1)} %copy-done.1, f32[256,576]{0,1:T(8,128)} %param.17, f32[256,576]{0,1:T(8,128)} %fusion.23, bf16[1024,640]{1,0:T(8,128)(2,1)S(1)} %bitcast.45, s32[1024]{0:T(1024)S(1)} %add_reduce_fusion), kind=kOutput, calls=%fused_computation.26 | convolution fusion | flops 303431680 | bytes 4263936 | tf_op jit(solution)/shard_map/dot_general | solution.py:310
  210.3 6.8 %all-to-all-done.3 = bf16[32,144,128]{2,1,0:T(8,128)(2,1)} async-done(((bf16[32,144,128]{2,1,0:T(8,128)(2,1)}), bf16[32,144,128]{2,1,0:T(8,128)(2,1)}, u32[]{:S(2)}, u32[]{:S(2)}) %all-to-all-start.3) | async-done | bytes 1179680 | tf_op jit(solution)/shard_map/all_to_all | solution.py:25
  217.1 1.4 reduce_sum.43
  218.5 5.7 %collective-permute-start.7 = (bf16[144,128]{1,0:T(8,128)(2,1)S(1)}, bf16[144,128]{1,0:T(8,128)(2,1)S(1)}, u32[]{:S(2)}, u32[]{:S(2)}) collective-permute-start(bf16[144,128]{1,0:T(8,128)(2,1)S(1)} %reduce_sum.43), channel_id=1, source_target_pairs={{0,0},{1,1},{2,2},{3,3},{4,32},{5,33},{6,34},{7,35},{8,64},{9,65},... | collective-permute-start | bytes 110600 | tf_op jit(solution)/shard_map/ppermute | solution.py:286
  224.2 3.9 %fusion.20 = f32[256,576]{0,1:T(8,128)} fusion(bf16[2304,576]{0,1:T(8,128)(2,1)} %param.10, s32[2304]{0:T(1024)S(1)} %add_bitcast_fusion, pred[2304]{0:T(1024)(128)(4,1)S(1)} %broadcast_compare_fusion, f32[256,576]{0,1:T(8,128)} %get-tuple-element.43, f32[256,576]{0,1:T(8,128)} %get-tuple-element.42), kind=kOutput, calls=%fused_computation.15 | convolution fusion | flops 681541632 | bytes 4435200 | tf_op jit(solution)/shard_map/dot_general | solution.py:299
  228.1 3.8 %collective-permute-done.7 = bf16[144,128]{1,0:T(8,128)(2,1)S(1)} collective-permute-done((bf16[144,128]{1,0:T(8,128)(2,1)S(1)}, bf16[144,128]{1,0:T(8,128)(2,1)S(1)}, u32[]{:S(2)}, u32[]{:S(2)}) %collective-permute-start.7) | collective-permute-done | bytes 36896 | tf_op jit(solution)/shard_map/ppermute | solution.py:286
  231.9 0.7 copy.39
  (54 shorter events, 0.8 us)
Async XLA Ops:
  7.2 1.3 copy-start
  7.2 92.2 %all-gather.3.cloned.1.call-start = ((), (), s32[]{:S(2)}) async-start(), calls=%async_computation.6 | async-start | bytes 9732096 | tf_op jit(solution)/shard_map/all_gather | solution.py:229
  30.6 148.4 %all-gather.5.cloned.1.call-start = ((), (), s32[]{:S(2)}) async-start(), calls=%async_computation.7 | async-start | bytes 5308416 | tf_op jit(solution)/shard_map/all_gather | solution.py:251
  35.3 15.1 %collective-permute-start = (bf16[1296,128]{1,0:T(8,128)(2,1)}, bf16[1296,128]{1,0:T(8,128)(2,1)S(1)}, u32[]{:S(2)}, u32[]{:S(2)}) collective-permute-start(bf16[1296,128]{1,0:T(8,128)(2,1)} %get-tuple-element.16), channel_id=1, source_target_pairs={{0,32},{32,64},{64,96},{96,128},{128,160},{160,192},{192,224},{224... | collective-permute-start | bytes 995336 | tf_op jit(solution)/shard_map/ppermute | solution.py:135
  35.7 31.7 %collective-permute-start.1 = (bf16[1296,128]{1,0:T(8,128)(2,1)}, bf16[1296,128]{1,0:T(8,128)(2,1)S(1)}, u32[]{:S(2)}, u32[]{:S(2)}) collective-permute-start(bf16[1296,128]{1,0:T(8,128)(2,1)} %get-tuple-element.17), channel_id=1, source_target_pairs={{0,64},{32,96},{64,128},{96,160},{128,192},{160,224},{192,0},{224,... | collective-permute-start | bytes 995336 | tf_op jit(solution)/shard_map/ppermute | solution.py:135
  36.4 48.5 %collective-permute-start.2 = (bf16[1296,128]{1,0:T(8,128)(2,1)}, bf16[1296,128]{1,0:T(8,128)(2,1)S(1)}, u32[]{:S(2)}, u32[]{:S(2)}) collective-permute-start(bf16[1296,128]{1,0:T(8,128)(2,1)} %get-tuple-element.18), channel_id=1, source_target_pairs={{0,96},{32,128},{64,160},{96,192},{128,224},{160,0},{192,32},{224,... | collective-permute-start | bytes 995336 | tf_op jit(solution)/shard_map/ppermute | solution.py:135
  39.1 45.8 %collective-permute-start.3 = (bf16[1296,128]{1,0:T(8,128)(2,1)}, bf16[1296,128]{1,0:T(8,128)(2,1)S(1)}, u32[]{:S(2)}, u32[]{:S(2)}) collective-permute-start(bf16[1296,128]{1,0:T(8,128)(2,1)} %get-tuple-element.19), channel_id=1, source_target_pairs={{0,128},{32,160},{64,192},{96,224},{128,0},{160,32},{192,64},{224,... | collective-permute-start | bytes 995336 | tf_op jit(solution)/shard_map/ppermute | solution.py:135
  42.1 42.8 %collective-permute-start.4 = (bf16[1296,128]{1,0:T(8,128)(2,1)}, bf16[1296,128]{1,0:T(8,128)(2,1)S(1)}, u32[]{:S(2)}, u32[]{:S(2)}) collective-permute-start(bf16[1296,128]{1,0:T(8,128)(2,1)} %get-tuple-element.20), channel_id=1, source_target_pairs={{0,160},{32,192},{64,224},{96,0},{128,32},{160,64},{192,96},{224,1... | collective-permute-start | bytes 995336 | tf_op jit(solution)/shard_map/ppermute | solution.py:135
  50.4 49.0 %copy-start.3 = (bf16[1296,128]{1,0:T(8,128)(2,1)}, bf16[1296,128]{1,0:T(8,128)(2,1)S(1)}, u32[]{:S(2)}) copy-start(bf16[1296,128]{1,0:T(8,128)(2,1)S(1)} %collective-permute-done.refs_1_) | copy-start | bytes 995332
  50.4 43.5 %collective-permute-start.5 = (bf16[1296,128]{1,0:T(8,128)(2,1)}, bf16[1296,128]{1,0:T(8,128)(2,1)}, u32[]{:S(2)}, u32[]{:S(2)}) collective-permute-start(bf16[1296,128]{1,0:T(8,128)(2,1)} %get-tuple-element.21), channel_id=1, source_target_pairs={{0,192},{32,224},{64,0},{96,32},{128,64},{160,96},{192,128},{224,1... | collective-permute-start | bytes 995336 | tf_op jit(solution)/shard_map/ppermute | solution.py:135
  67.4 32.0 %copy-start.4 = (bf16[1296,128]{1,0:T(8,128)(2,1)}, bf16[1296,128]{1,0:T(8,128)(2,1)S(1)}, u32[]{:S(2)}) copy-start(bf16[1296,128]{1,0:T(8,128)(2,1)S(1)} %collective-permute-done.1.refs_2_) | copy-start | bytes 995332
  67.4 32.0 %collective-permute-start.6 = (bf16[1296,128]{1,0:T(8,128)(2,1)}, bf16[1296,128]{1,0:T(8,128)(2,1)}, u32[]{:S(2)}, u32[]{:S(2)}) collective-permute-start(bf16[1296,128]{1,0:T(8,128)(2,1)} %get-tuple-element.22), channel_id=1, source_target_pairs={{0,224},{32,0},{64,32},{96,64},{128,96},{160,128},{192,160},{224,1... | collective-permute-start | bytes 995336 | tf_op jit(solution)/shard_map/ppermute | solution.py:135
  84.9 14.5 %copy-start.5 = (bf16[1296,128]{1,0:T(8,128)(2,1)}, bf16[1296,128]{1,0:T(8,128)(2,1)S(1)}, u32[]{:S(2)}) copy-start(bf16[1296,128]{1,0:T(8,128)(2,1)S(1)} %collective-permute-done.2.refs_3_) | copy-start | bytes 995332
  84.9 14.5 %copy-start.6 = (bf16[1296,128]{1,0:T(8,128)(2,1)}, bf16[1296,128]{1,0:T(8,128)(2,1)S(1)}, u32[]{:S(2)}) copy-start(bf16[1296,128]{1,0:T(8,128)(2,1)S(1)} %collective-permute-done.3.refs_4_) | copy-start | bytes 995332
  84.9 14.4 %copy-start.7 = (bf16[1296,128]{1,0:T(8,128)(2,1)}, bf16[1296,128]{1,0:T(8,128)(2,1)S(1)}, u32[]{:S(2)}) copy-start(bf16[1296,128]{1,0:T(8,128)(2,1)S(1)} %collective-permute-done.4.refs_5_) | copy-start | bytes 995332
  99.4 13.2 %copy-start.10 = (s32[1,2,24,1]{2,3,1,0:T(1,128)S(1)}, s32[1,2,24,1]{2,3,1,0:T(1,128)}, u32[]{:S(2)}) copy-start(s32[1,2,24,1]{2,3,1,0:T(1,128)} %param.14) | copy-start | bytes 580
  99.4 14.0 %copy-start.11 = (s32[1,2,24]{2,1,0:T(2,128)S(1)}, s32[1,2,24]{2,1,0:T(2,128)}, u32[]{:S(2)}) copy-start(s32[1,2,24]{2,1,0:T(2,128)} %param.15) | copy-start | bytes 580
  99.4 14.1 %copy-start.2 = (bf16[1,2,24,4608]{3,2,1,0:T(8,128)(2,1)S(1)}, bf16[1,2,24,4608]{3,2,1,0:T(8,128)(2,1)}, u32[]{:S(2)}) copy-start(bf16[1,2,24,4608]{3,2,1,0:T(8,128)(2,1)} %param.13) | copy-start | bytes 1327108
  112.1 8.3 %copy-start.8 = (s32[2304]{0:T(1024)S(1)}, s32[2304]{0:T(1024)}, u32[]{:S(2)}) copy-start(s32[2304]{0:T(1024)} %param.11) | copy-start | bytes 27652
  112.1 28.4 %copy-start.9 = (f32[2,1024]{1,0:T(2,128)S(1)}, f32[2,1024]{1,0:T(2,128)}, u32[]{:S(2)}) copy-start(f32[2,1024]{1,0:T(2,128)} %get-tuple-element.23) | copy-start | bytes 24580
  114.9 25.2 %all-to-all-start.4 = ((bf16[8,48,640]{2,1,0:T(8,128)(2,1)}), bf16[8,48,640]{2,1,0:T(8,128)(2,1)S(1)}, u32[]{:S(2)}, u32[]{:S(2)}) async-start(bf16[8,48,640]{2,1,0:T(8,128)(2,1)} %copy.37), calls=%async_computation.4 | async-start | bytes 983040 | tf_op jit(solution)/shard_map/all_to_all | solution.py:25
  141.2 14.7 %all-to-all-start.1 = ((f32[32,16,128]{2,1,0:T(8,128)}), f32[32,16,128]{2,1,0:T(8,128)S(1)}, u32[]{:S(2)}, u32[]{:S(2)}) async-start(f32[32,16,128]{2,1,0:T(8,128)} %broadcast_in_dim.60), calls=%async_computation.1 | async-start | bytes 524288 | tf_op jit(solution)/shard_map/all_to_all | solution.py:19
  156.6 13.3 %all-to-all-start.2 = ((f32[8,16,128]{2,1,0:T(8,128)}), f32[8,16,128]{2,1,0:T(8,128)S(1)}, u32[]{:S(2)}, u32[]{:S(2)}) async-start(f32[8,16,128]{2,1,0:T(8,128)} %broadcast_in_dim.61), calls=%async_computation.2 | async-start | bytes 131072 | tf_op jit(solution)/shard_map/all_to_all | solution.py:19
  170.0 24.1 %all-to-all-start.5 = ((bf16[32,32,640]{2,1,0:T(8,128)(2,1)}), bf16[32,32,640]{2,1,0:T(8,128)(2,1)S(1)}, u32[]{:S(2)}, u32[]{:S(2)}) async-start(bf16[32,32,640]{2,1,0:T(8,128)(2,1)} %bitcast.50), calls=%async_computation.5 | async-start | bytes 2621440 | tf_op jit(solution)/shard_map/all_to_all | solution.py:25
  194.1 23.0 %all-to-all-start.3 = ((bf16[32,144,128]{2,1,0:T(8,128)(2,1)}), bf16[32,144,128]{2,1,0:T(8,128)(2,1)}, u32[]{:S(2)}, u32[]{:S(2)}) async-start(bf16[32,144,128]{2,1,0:T(8,128)(2,1)} %bitcast.46), calls=%async_computation.3 | async-start | bytes 2359296 | tf_op jit(solution)/shard_map/all_to_all | solution.py:25
  201.4 6.0 %copy-start.1 = (f32[256,576]{0,1:T(8,128)S(1)}, f32[256,576]{0,1:T(8,128)}, u32[]{:S(2)}) copy-start(f32[256,576]{0,1:T(8,128)} %param.16) | copy-start | bytes 1769476
  218.5 13.4 %collective-permute-start.7 = (bf16[144,128]{1,0:T(8,128)(2,1)S(1)}, bf16[144,128]{1,0:T(8,128)(2,1)S(1)}, u32[]{:S(2)}, u32[]{:S(2)}) collective-permute-start(bf16[144,128]{1,0:T(8,128)(2,1)S(1)} %reduce_sum.43), channel_id=1, source_target_pairs={{0,0},{1,1},{2,2},{3,3},{4,32},{5,33},{6,34},{7,35},{8,64},{9,65},... | collective-permute-start | bytes 110600 | tf_op jit(solution)/shard_map/ppermute | solution.py:286
Sparse Core Ops, SparseCore 0:
  30.8 57.3 all-gather.2
  112.2 66.7 all-gather.4
